TPU v7x, 32 devices: a whole 2x2x4 slice. The times are simulated.
32 devices in a mesh: dp: 8 (over z, core), tp: 4 (over y, x).
Axes of the slice: x: 2, y: 2, z: 4, core: 2. Of those that a mesh axis runs over, the one named last changes fastest.
Arguments:
- tokens: bfloat16 [4096, 4096], P('dp'), may hold values from -6 to 6
- gain: float32 [4096], replicated, may hold values from 0.1 to 1.9
- router: float32 [4096, 8], replicated, may hold values from -0.09375 to 0.09375
- routes: int32 [4096, 2], P('dp'), may hold values from 0 to 7, all different within a row
- w_gate: bfloat16 [2, 4096, 1024], P(None, 'dp', 'tp'), may hold values from -0.125 to 0.125
- w_up: bfloat16 [2, 4096, 1024], P(None, 'dp', 'tp'), may hold values from -0.125 to 0.125
- w_down: bfloat16 [2, 1024, 4096], P(None, 'dp', 'tp'), may hold values from -0.25 to 0.25
Outputs:
- mixed: bfloat16 [4096, 4096], P('dp', 'tp')
Inputs may be any that keep to these rules, and one draw needn't show every extreme that they name: `routes`: each row names two different experts.
All inputs are finite; a program needn't handle non-finite values.
Results may differ from a plain program's by a relative error of at most 0.0065.
Values may be sent and summed in bfloat16 or wider, within the bound.
A program may use at most 64 MiB of HBM per device.

v0:
```python
import jax
import jax.numpy as jnp
from jax import lax
from jax.sharding import PartitionSpec as P

EPS = 1e-06
ROUTE_SCALE = 2.5


def per_device(tokens, gain, router, routes, w_gate, w_up, w_down):
    values = tokens.astype(jnp.float32)
    square = jnp.mean(values * values, axis=-1, keepdims=True)
    normed = (values * lax.rsqrt(square + EPS) * gain).astype(jnp.bfloat16)
    scores = jax.nn.sigmoid(
        jnp.dot(normed.astype(jnp.float32), router, precision=lax.Precision.HIGHEST)
    )
    labels = jnp.arange(router.shape[1], dtype=jnp.int32)
    picked_mask = (routes[:, :, None] == labels[None, None, :]).astype(jnp.float32)
    picked = jnp.sum(picked_mask * scores[:, None, :], axis=-1)
    chosen = jnp.sum(picked_mask, axis=1)
    combine = chosen * scores * ROUTE_SCALE / jnp.sum(picked, axis=-1, keepdims=True)
    held_weights = combine[:, : w_gate.shape[0]]
    full_gate, full_up, full_down = (
        lax.all_gather(w_gate, "dp", axis=1, tiled=True),
        lax.all_gather(w_up, "dp", axis=1, tiled=True),
        lax.all_gather(w_down, "dp", axis=1, tiled=True),
    )
    gate_value = jnp.einsum("td,edf->tef", normed, full_gate, preferred_element_type=jnp.float32)
    up_value = jnp.einsum("td,edf->tef", normed, full_up, preferred_element_type=jnp.float32)
    hidden = (jax.nn.silu(gate_value) * up_value * held_weights[:, :, None]).astype(jnp.bfloat16)
    whole_hidden = lax.all_gather(hidden, "tp", axis=2, tiled=True)
    mixed = jnp.einsum("tef,efd->td", whole_hidden, full_down, preferred_element_type=jnp.float32)
    return mixed.astype(jnp.bfloat16)


def solution(mesh):
    return jax.shard_map(
        per_device,
        mesh=mesh,
        in_specs=(
            P("dp", None),
            P(),
            P(),
            P("dp", None),
            P(None, "dp", "tp"),
            P(None, "dp", "tp"),
            P(None, "dp", "tp"),
        ),
        out_specs=P("dp", "tp"),
        check_vma=False,
    )
```

profile of v0, /device:TPU:0, one launch (start us, length us, event | category | flops | bytes accessed | tf_op | source)
XLA Modules:
  0.0 201.4 jit_solution(2412415738272658088)
XLA Ops:
  6.5 0.0 copy-start
  6.5 0.0 copy-start.3
  6.5 0.0 all-gather.5.cloned.1.call-start
  6.5 0.7 all-gather.5.cloned.1.call-update
  7.3 0.0 all-gather.7.cloned.1.call-start
  7.3 0.7 all-gather.7.cloned.1.call-update
  8.0 0.0 all-gather.11.cloned.1.call-start
  8.1 0.7 all-gather.11.cloned.1.call-update
  8.7 0.0 all-gather.9.cloned.1.call-start
  8.8 0.0 copy-start.1
  8.8 3.2 %fusion = f32[512]{0:T(512)S(1)} fusion(bf16[512,4096]{1,0:T(8,128)(2,1)} %param.7), kind=kLoop, calls=%fused_computation.2 | loop fusion | flops 6290944 | bytes 4196352 | tf_op jit(solution)/shard_map/reduce_sum | solution.py:12
  12.0 0.0 copy-start.2
  12.1 0.0 copy-done
  12.1 0.0 copy-done.3
  12.1 0.2 copy-done.1
  12.2 3.4 %fusion.18 = f32[512,8]{0,1:T(8,128)S(1)} fusion(f32[4096,8]{0,1:T(8,128)S(1)} %copy-done, bf16[512,4096]{1,0:T(8,128)(2,1)S(1)} %copy-done.1, f32[4096]{0:T(1024)S(1)} %copy-done.3, f32[512]{0:T(512)S(1)} %add_rsqrt_fusion), kind=kOutput, calls=%fused_computation.16 | convolution fusion | flops 209727488 | bytes 4360192 | tf_op jit(solution)/shard_map/dot_general | solution.py:15
  15.7 0.0 copy-done.2
  15.7 42.8 %all-gather.5.cloned.1.call-done = bf16[2,4096,256]{2,1,0:T(8,128)(2,1)} async-done(((bf16[2,512,256]{2,1,0:T(8,128)(2,1)}), bf16[2,4096,256]{2,1,0:T(8,128)(2,1)}) %all-gather.5.cloned.1.call-update) | async-done | bytes 4194320 | tf_op jit(solution)/shard_map/all_gather | solution.py:24
  58.6 5.8 %fusion.5 = f32[512,2,256]{2,0,1:T(8,128)S(1)} fusion(bf16[2,4096,256]{2,1,0:T(8,128)(2,1)} %all-gather.5.cloned.1.call-done, bf16[512,4096]{1,0:T(8,128)(2,1)} %param.7, f32[4096]{0:T(1024)S(1)} %copy-done.3, f32[512]{0:T(512)S(1)} %add_rsqrt_fusion), kind=kOutput, calls=%fused_computation.7 | convolution fusion | flops 2155872256 | bytes 9455616 | tf_op jit(solution)/shard_map/td,edf->tef/dot_general | solution.py:28
  64.4 41.5 %all-gather.7.cloned.1.call-done = bf16[2,4096,256]{2,1,0:T(8,128)(2,1)} async-done(((bf16[2,512,256]{2,1,0:T(8,128)(2,1)}), bf16[2,4096,256]{2,1,0:T(8,128)(2,1)}) %all-gather.7.cloned.1.call-update) | async-done | bytes 4194320 | tf_op jit(solution)/shard_map/all_gather | solution.py:25
  105.9 6.8 %fusion.13 = bf16[512,2,256]{2,0,1:T(8,128)(2,1)} fusion(bf16[2,4096,256]{2,1,0:T(8,128)(2,1)} %all-gather.7.cloned.1.call-done, f32[512,2,256]{2,0,1:T(8,128)S(1)} %fusion.5, f32[512,2]{0,1:T(2,128)S(1)} %fusion.20, bf16[512,4096]{1,0:T(8,128)(2,1)} %param.7, f32[4096]{0:T(1024)S(1)} %copy-done.3, f32[512]{0:T(512)S(1)} %add_rsqrt_fusion), kind=kOutput, calls=%fused_computation.12 | convolution fusion | flops 2157707264 | bytes 9984000 | tf_op jit(solution)/shard_map/td,edf->tef/dot_general | solution.py:29
  112.6 0.0 all-gather.9.cloned.1.call-update
  112.7 40.5 %all-gather.11.cloned.1.call-done = bf16[2,1024,1024]{2,1,0:T(8,128)(2,1)} async-done(((bf16[2,128,1024]{2,1,0:T(8,128)(2,1)}), bf16[2,1024,1024]{2,1,0:T(8,128)(2,1)}) %all-gather.11.cloned.1.call-update) | async-done | bytes 4194320 | tf_op jit(solution)/shard_map/all_gather | solution.py:26
  153.2 35.6 %all-gather.9.cloned.1.call-done = bf16[512,2,1024]{2,0,1:T(8,128)(2,1)} async-done(((bf16[512,2,256]{2,0,1:T(8,128)(2,1)}), bf16[512,2,1024]{2,0,1:T(8,128)(2,1)}) %all-gather.9.cloned.1.call-update) | async-done | bytes 2097168 | tf_op jit(solution)/shard_map/all_gather | solution.py:31
  188.8 6.1 %bitcast_convert_fusion = bf16[512,1024]{1,0:T(8,128)(2,1)} fusion(bf16[512,2,1024]{2,0,1:T(8,128)(2,1)} %all-gather.9.cloned.1.call-done, bf16[2,1024,1024]{2,1,0:T(8,128)(2,1)} %all-gather.11.cloned.1.call-done), kind=kOutput, calls=%fused_computation.9 | convolution fusion | flops 2148007936 | bytes 7340032 | tf_op jit(solution)/shard_map/tef,efd->td/dot_general | solution.py:32
  (3 shorter events, 0.0 us)
Async XLA Ops:
  6.5 5.5 %copy-start = (f32[4096,8]{0,1:T(8,128)S(1)}, f32[4096,8]{0,1:T(8,128)}, u32[]{:S(2)}) copy-start(f32[4096,8]{0,1:T(8,128)} %param.9) | copy-start | bytes 393220
  6.5 5.5 %copy-start.3 = (f32[4096]{0:T(1024)S(1)}, f32[4096]{0:T(1024)}, u32[]{:S(2)}) copy-start(f32[4096]{0:T(1024)} %param.8) | copy-start | bytes 49156
  6.5 52.0 %all-gather.5.cloned.1.call-start = ((), (), s32[]{:S(2)}) async-start(), calls=%async_computation | async-start | bytes 4718592 | tf_op jit(solution)/shard_map/all_gather | solution.py:24
  7.3 98.6 %all-gather.7.cloned.1.call-start = ((), (), s32[]{:S(2)}) async-start(), calls=%async_computation.1 | async-start | bytes 4718592 | tf_op jit(solution)/shard_map/all_gather | solution.py:25
  8.0 145.2 %all-gather.11.cloned.1.call-start = ((), (), s32[]{:S(2)}) async-start(), calls=%async_computation.3 | async-start | bytes 4718592 | tf_op jit(solution)/shard_map/all_gather | solution.py:26
  8.7 180.0 %all-gather.9.cloned.1.call-start = ((), (), s32[]{:S(2)}) async-start(), calls=%async_computation.2 | async-start | bytes 2621440 | tf_op jit(solution)/shard_map/all_gather | solution.py:31
  8.8 3.5 %copy-start.1 = (bf16[512,4096]{1,0:T(8,128)(2,1)S(1)}, bf16[512,4096]{1,0:T(8,128)(2,1)}, u32[]{:S(2)}) copy-start(bf16[512,4096]{1,0:T(8,128)(2,1)} %param.7) | copy-start | bytes 12582916
  12.0 3.6 %copy-start.2 = (s32[512,2]{0,1:T(2,128)S(1)}, s32[512,2]{0,1:T(2,128)}, u32[]{:S(2)}) copy-start(s32[512,2]{0,1:T(2,128)} %param.10) | copy-start | bytes 12292
Sparse Core Ops, SparseCore 0:
  8.9 49.5 all-gather.4
  60.2 45.6 all-gather.6
  107.5 45.6 all-gather.10
  154.9 33.8 all-gather.8
where the time goes:
time: 202 us; the launch traced here: 201 us
  waiting for transfers between devices  162 us (80%)
  matrix products  22.2 us (11%)
  between operations  13.2 us (7%)
  other arithmetic  3.27 us (2%)
    all_gather x1, waiting for transfers between devices, per_device(): lax.all_gather(w_gate, 'dp', axis=1, tiled=True)  42.8 us
    all_gather x1, waiting for transfers between devices, per_device(): lax.all_gather(w_up, 'dp', axis=1, tiled=True)  41.5 us
    all_gather x1, waiting for transfers between devices, per_device(): lax.all_gather(w_down, 'dp', axis=1, tiled=True)  40.5 us
    all_gather x1, waiting for transfers between devices, per_device(): whole_hidden = lax.all_gather(hidden, 'tp', axis=2, tiled=True)  35.6 us
    dot_general x1, matrix products, per_device(): jnp.einsum('td,edf->tef', normed, full_up, preferred_element_type=jnp.flo...  6.76 us
    dot_general x1, matrix products, per_device(): jnp.einsum('tef,efd->td', whole_hidden, full_down, preferred_element_type...  6.12 us
    dot_general x1, matrix products, per_device(): jnp.einsum('td,edf->tef', normed, full_gate, preferred_element_type=jnp.f...  5.84 us
  transfers between devices with their start and end apart: 4, of which 4 were waited for; matrix products, arithmetic and copies ran while one was open for 10% of the time, Pallas kernels for 0%

commit v1 on v0

--- a/solution.py
+++ b/solution.py
@@ -1,13 +1,19 @@
+import functools
+
 import jax
 import jax.numpy as jnp
 from jax import lax
+from jax.experimental import pallas as pl
+from jax.experimental.pallas import tpu as pltpu
 from jax.sharding import PartitionSpec as P
 
 EPS = 1e-06
 ROUTE_SCALE = 2.5
-
-
-def per_device(tokens, gain, router, routes, w_gate, w_up, w_down):
+MESH = pl.DeviceIdType.MESH
+CORES = 2
+
+
+def gathered(tokens, gain, router, routes, w_gate, w_up, w_down):
     values = tokens.astype(jnp.float32)
     square = jnp.mean(values * values, axis=-1, keepdims=True)
     normed = (values * lax.rsqrt(square + EPS) * gain).astype(jnp.bfloat16)
@@ -33,9 +39,276 @@
     return mixed.astype(jnp.bfloat16)
 
 
+def kernel(
+    groups, tps, x_hbm, gain_ref, router_ref, routes_ref, wg_hbm, wu_hbm, wd_hbm, o_ref,
+    x, w, dn, hid, comb,
+    x_sem, own_sem, recv_sem, up_sem, down_sem, side_sem, hid_send, hid_recv,
+):
+    dp, tp = lax.axis_index("dp"), lax.axis_index("tp")
+    positions = groups // CORES
+    z, core = dp // CORES, dp % CORES
+    experts = wg_hbm.shape[0]
+    rows = x.shape[0]
+    top, bottom = z == positions - 1, z == 0
+    above = (jnp.minimum(z + 1, positions - 1) * CORES + core, tp)
+    below = (jnp.maximum(z - 1, 0) * CORES + core, tp)
+    side = (z * CORES + (1 - core), tp)
+
+    load_x = pltpu.make_async_copy(x_hbm, x, x_sem)
+    load_x.start()
+    chunks = [(m, e) for e in range(experts) for m in (0, 1)] + [(2, e) for e in range(experts)]
+
+    def source(k):
+        m, e = chunks[k]
+        return (wg_hbm, wu_hbm, wd_hbm)[m].at[e]
+
+    def slot(k, d):
+        m, e = chunks[k]
+        return dn.at[e, d] if m == 2 else w.at[m, e, d]
+
+    def copy_own(k):
+        return pltpu.make_async_copy(source(k), slot(k, dp), own_sem.at[k])
+
+    for k in range(len(chunks)):
+        copy_own(k).start()
+
+    barrier = pltpu.get_barrier_semaphore()
+    pl.semaphore_signal(barrier, inc=1, device_id=side, device_id_type=MESH)
+    for i in range(1, tps):
+        pl.semaphore_signal(
+            barrier, inc=1, device_id=(dp, lax.rem(tp + i, tps)), device_id_type=MESH
+        )
+
+    @pl.when(jnp.logical_not(top))
+    def _():
+        pl.semaphore_signal(barrier, inc=1, device_id=above, device_id_type=MESH)
+
+    @pl.when(jnp.logical_not(bottom))
+    def _():
+        pl.semaphore_signal(barrier, inc=1, device_id=below, device_id_type=MESH)
+
+    ends = jnp.where(top, 1, 0) + jnp.where(bottom, 1, 0)
+    pl.semaphore_wait(barrier, tps + 2 - ends)
+
+    def send(k, d, src, sem, to):
+        return pltpu.make_async_remote_copy(
+            src_ref=src, dst_ref=slot(k, d), send_sem=sem.at[k, d // CORES],
+            recv_sem=recv_sem.at[k, d], device_id=to, device_id_type=MESH,
+        )
+
+    def arrived(k, d):
+        pltpu.make_async_remote_copy(
+            src_ref=slot(k, d), dst_ref=slot(k, d), send_sem=side_sem.at[k, d // CORES],
+            recv_sem=recv_sem.at[k, d], device_id=side, device_id_type=MESH,
+        ).wait_recv()
+
+    def send_own(k):
+        @pl.when(jnp.logical_not(top))
+        def _():
+            send(k, dp, source(k), up_sem, above).start()
+
+        @pl.when(jnp.logical_not(bottom))
+        def _():
+            send(k, dp, source(k), down_sem, below).start()
+
+        send(k, dp, source(k), side_sem, side).start()
+
+    def relay(k):
+        for j in range(1, positions):
+            @pl.when(z - j >= 0)
+            def _():
+                d = dp - j * CORES
+                arrived(k, d)
+
+                @pl.when(jnp.logical_not(top))
+                def _():
+                    send(k, d, slot(k, d), up_sem, above).start()
+
+                send(k, d, slot(k, d), side_sem, side).start()
+
+            @pl.when(z + j <= positions - 1)
+            def _():
+                d = dp + j * CORES
+                arrived(k, d)
+
+                @pl.when(jnp.logical_not(bottom))
+                def _():
+                    send(k, d, slot(k, d), down_sem, below).start()
+
+                send(k, d, slot(k, d), side_sem, side).start()
+
+    def wait_side(k):
+        for p in range(positions):
+            arrived(k, p * CORES + (1 - core))
+        copy_own(k).wait()
+
+    def norm():
+        step = rows // 8
+
+        def body(i, _):
+            part = pl.ds(pl.multiple_of(i * step, step), step)
+            v = x[part, :].astype(jnp.float32)
+            square = jnp.mean(v * v, axis=-1, keepdims=True)
+            x[part, :] = (v * lax.rsqrt(square + EPS) * gain_ref[...]).astype(jnp.bfloat16)
+            return 0
+
+        lax.fori_loop(0, 8, body, 0)
+
+    def score():
+        rest = router_ref[...]
+        total = jnp.zeros((rows, rest.shape[0]), jnp.float32)
+        parts = []
+        for _ in range(3):
+            part = rest.astype(jnp.bfloat16)
+            rest = rest - part.astype(jnp.float32)
+            parts.append(part)
+        for part in parts[::-1]:
+            total += lax.dot_general(
+                x[...], part, (((1,), (1,)), ((), ())), preferred_element_type=jnp.float32
+            )
+        scores = 1.0 / (1.0 + jnp.exp(-total))
+        routed = scores.shape[1]
+        picks = routes_ref[...].astype(jnp.float32)
+        labels = lax.broadcasted_iota(jnp.int32, scores.shape, 1).astype(jnp.float32)
+        chosen = jnp.zeros_like(scores)
+        for i in range(routes_ref.shape[0]):
+            column = jnp.transpose(jnp.broadcast_to(picks[i : i + 1, :], (128, rows)))
+            chosen += jnp.where(column[:, :routed] == labels, 1.0, 0.0)
+        picked = chosen * scores
+        comb[...] = picked * ROUTE_SCALE / jnp.sum(picked, axis=-1, keepdims=True)
+
+    def send_hidden(e, i):
+        return pltpu.make_async_remote_copy(
+            src_ref=hid.at[e, tp], dst_ref=hid.at[e, tp], send_sem=hid_send.at[e, i - 1],
+            recv_sem=hid_recv.at[e, tp],
+            device_id=(dp, lax.rem(tp + i, tps)), device_id_type=MESH,
+        )
+
+    def experts_hidden(e):
+        step = rows // 2
+
+        def body(i, _):
+            part = pl.ds(pl.multiple_of(i * step, step), step)
+            lhs = x[part, :]
+            depth = x.shape[1]
+            gate = jnp.dot(
+                lhs, w[0, e].reshape(depth, w.shape[-1]), preferred_element_type=jnp.float32
+            )
+            up = jnp.dot(
+                lhs, w[1, e].reshape(depth, w.shape[-1]), preferred_element_type=jnp.float32
+            )
+            hid[e, tp, part, :] = (gate / (1.0 + jnp.exp(-gate)) * up).astype(jnp.bfloat16)
+            return 0
+
+        lax.fori_loop(0, 2, body, 0)
+        for i in range(1, tps):
+            send_hidden(e, i).start()
+
+    def down():
+        cols = o_ref.shape[1]
+        step = cols // 4
+
+        def body(i, _):
+            part = pl.ds(pl.multiple_of(i * step, step), step)
+            total = None
+            for e in range(experts):
+                lhs = jnp.concatenate([hid[e, t] for t in range(tps)], axis=1)
+                rhs = dn[e, :, :, part].reshape(lhs.shape[1], step)
+                term = jnp.dot(lhs, rhs, preferred_element_type=jnp.float32)
+                term = term * comb[:, e : e + 1]
+                total = term if total is None else total + term
+            o_ref[:, part] = total.astype(o_ref.dtype)
+            return 0
+
+        lax.fori_loop(0, 4, body, 0)
+
+    ahead = 2
+    for k in range(min(ahead, len(chunks))):
+        send_own(k)
+    for k in range(len(chunks)):
+        relay(k)
+        if k + ahead < len(chunks):
+            send_own(k + ahead)
+        m, e = chunks[k]
+        if k == 0:
+            load_x.wait()
+            norm()
+        if k == 2:
+            score()
+        if m == 1:
+            wait_side(k - 1)
+            wait_side(k)
+            experts_hidden(e)
+    for k, (m, e) in enumerate(chunks):
+        if m == 2:
+            wait_side(k)
+    for e in range(experts):
+        for i in range(1, tps):
+            s = lax.rem(tp + i, tps)
+            pltpu.make_async_remote_copy(
+                src_ref=hid.at[e, s], dst_ref=hid.at[e, s], send_sem=hid_send.at[e, i - 1],
+                recv_sem=hid_recv.at[e, s], device_id=side, device_id_type=MESH,
+            ).wait_recv()
+    down()
+
+    for e in range(experts):
+        for i in range(1, tps):
+            send_hidden(e, i).wait_send()
+    for k in range(len(chunks)):
+        for p in range(positions):
+            d = p * CORES + core
+            send(k, d, slot(k, d), side_sem, side).wait_send()
+
+            @pl.when(jnp.logical_and(jnp.logical_not(top), p <= z))
+            def _():
+                send(k, d, slot(k, d), up_sem, above).wait_send()
+
+            @pl.when(jnp.logical_and(jnp.logical_not(bottom), p >= z))
+            def _():
+                send(k, d, slot(k, d), down_sem, below).wait_send()
+
+
+def streamed(groups, tps, tokens, gain, router, routes, w_gate, w_up, w_down):
+    rows, depth = tokens.shape
+    experts, shard, width = w_gate.shape
+    down_rows, cols = w_down.shape[1:]
+    positions = groups // CORES
+    vmem = pl.BlockSpec(memory_space=pltpu.VMEM)
+    hbm = pl.BlockSpec(memory_space=pl.ANY)
+    chunks = 3 * experts
+    dma = pltpu.SemaphoreType.DMA
+    return pl.pallas_call(
+        functools.partial(kernel, groups, tps),
+        out_shape=jax.ShapeDtypeStruct((rows, cols), jnp.bfloat16),
+        in_specs=[hbm, vmem, vmem, vmem, hbm, hbm, hbm],
+        out_specs=vmem,
+        scratch_shapes=[
+            pltpu.VMEM((rows, depth), jnp.bfloat16),
+            pltpu.VMEM((2, experts, groups, shard, width), jnp.bfloat16),
+            pltpu.VMEM((experts, groups, down_rows, cols), jnp.bfloat16),
+            pltpu.VMEM((experts, tps, rows, width), jnp.bfloat16),
+            pltpu.VMEM((rows, router.shape[1]), jnp.float32),
+            dma,
+            dma((chunks,)),
+            dma((chunks, groups)),
+            dma((chunks, positions)),
+            dma((chunks, positions)),
+            dma((chunks, positions)),
+            dma((experts, tps - 1)),
+            dma((experts, tps)),
+        ],
+        compiler_params=pltpu.CompilerParams(
+            collective_id=0, has_side_effects=True, vmem_limit_bytes=60 * 1024 * 1024
+        ),
+    )(tokens, gain.reshape(1, -1), router.T, routes.T, w_gate, w_up, w_down)
+
+
 def solution(mesh):
+    groups, tps = mesh.shape["dp"], mesh.shape["tp"]
+    fits = groups % CORES == 0 and groups // CORES <= 4
+    body = functools.partial(streamed, groups, tps) if fits else gathered
     return jax.shard_map(
-        per_device,
+        body,
         mesh=mesh,
         in_specs=(
             P("dp", None),

time: 202 us -> 118 us (0.58)
  waiting for transfers between devices: 162 us -> 0 us
  Pallas kernels: 0 us -> 115 us
  matrix products: 22.2 us -> 0 us
  between operations: 13.2 us -> 0.01 us
  other arithmetic: 3.27 us -> 0 us
  local copies, waits for them, and re-layouts: 0.18 us -> 2.26 us
    all_gather x4 -> x0, waiting for transfers between devices: 160 us -> none  [the longest x1 42.8 us: per_device(): lax.all_gather(w_gate, 'dp', axis=1, tiled=True)]
    pallas_call x0 -> x1, Pallas kernels: none -> 115 us  [streamed(): pl.pallas_call(functools.partial(kernel, groups, tps), out_shape=jax.Shap...]
    dot_general x4 -> x0, matrix products: 22.2 us -> none  [the longest x1 6.76 us: per_device(): jnp.einsum('td,edf->tef', normed, full_up, preferred_element_type=jnp.flo...]
    reduce_sum x2 -> x0, other arithmetic: 3.26 us -> none  [the longest x1 3.23 us: per_device(): square = jnp.mean(values * values, axis=-1, keepdims=True)]
    unnamed x4 -> x0, waiting for transfers between devices: 2.1 us -> none
    unnamed x8 -> x1, local copies, waits for them, and re-layouts: 0.18 us -> 2.26 us
  transfers between devices with their start and end apart: 4 -> 0, of which waited for: 4 -> 0; matrix products, arithmetic and copies ran while one was open for 10% -> 0% of each run, Pallas kernels for 0% -> 0%
where the time goes in v1:
time: 118 us; the launch traced here: 117 us
  Pallas kernels  115 us (97%)
  local copies, waits for them, and re-layouts  2.26 us (2%)
    pallas_call x1, Pallas kernels, streamed(): pl.pallas_call(functools.partial(kernel, groups, tps), out_shape=jax.Shap...  115 us

profile of v1, /device:TPU:0, one launch (start us, length us, event | category | flops | bytes accessed | tf_op | source)
XLA Modules:
  0.0 117.2 jit_solution(17711538294319322564)
XLA Ops:
  0.0 114.9 %shard_map.73 = bf16[512,1024]{1,0:T(8,128)(2,1)} custom-call(bf16[512,4096]{1,0:T(8,128)(2,1)} %x_hbm.1, f32[1,4096]{1,0:T(1,128)} %bitcast.4, f32[8,4096]{1,0:T(8,128)} %bitcast.3, s32[2,512]{1,0:T(2,128)} %bitcast.5, bf16[2,512,256]{2,1,0:T(8,128)(2,1)} %wg_hbm.1, bf16[2,512,256]{2,1,0:T(8,128)(2,1)} %wu_hbm.1, bf16[2,128,1024]{2,1,0:T(8,128)(2,1)} %wd_hbm.1), custom_call_target="tpu_custom_call" | custom-call | tf_op jit(solution)/shard_map/pallas_call | solution.py:280
  114.9 2.3 %copy.9 = bf16[512,1024]{1,0:T(8,128)(2,1)} copy(bf16[512,1024]{1,0:T(8,128)(2,1)} %shard_map.73) | data formatting | bytes 2097152

commit v2 on v1

--- a/solution.py
+++ b/solution.py
@@ -11,6 +11,8 @@
 ROUTE_SCALE = 2.5
 MESH = pl.DeviceIdType.MESH
 CORES = 2
+PIECES = 4
+HOSTED = (0,)
 
 
 def gathered(tokens, gain, router, routes, w_gate, w_up, w_down):
@@ -40,23 +42,36 @@
 
 
 def kernel(
-    groups, tps, x_hbm, gain_ref, router_ref, routes_ref, wg_hbm, wu_hbm, wd_hbm, o_ref,
-    x, w, dn, hid, comb,
-    x_sem, own_sem, recv_sem, up_sem, down_sem, side_sem, hid_send, hid_recv,
+    groups, tps, hosted, x_hbm, gain_ref, router_ref, routes_ref, wg_hbm, wu_hbm, wd_hbm, o_ref,
+    x, guest, guest_normed, w, dn, hid, guest_hid, comb,
+    x_sem, own_sem, recv_sem, in_sem, out_sem, side_sem, hid_send, hid_recv,
+    tok_send, tok_recv, back_send, back_recv,
 ):
     dp, tp = lax.axis_index("dp"), lax.axis_index("tp")
     positions = groups // CORES
     z, core = dp // CORES, dp % CORES
     experts = wg_hbm.shape[0]
     rows = x.shape[0]
-    top, bottom = z == positions - 1, z == 0
-    above = (jnp.minimum(z + 1, positions - 1) * CORES + core, tp)
-    below = (jnp.maximum(z - 1, 0) * CORES + core, tp)
+    end = jnp.logical_or(z == positions - 1, z == 0)
+    out = 2 * (2 * z // positions) - 1
+
+    def at(p):
+        return (p * CORES + core, tp)
+
+    inner = at(z - out)
+    outer = at(jnp.clip(z + out, 0, positions - 1))
     side = (z * CORES + (1 - core), tp)
+    along_x = tp + 1 - 2 * (tp % 2)
+    along_y = lax.rem(tp + 2, tps)
+    across = lax.rem(along_x + 2, tps)
 
     load_x = pltpu.make_async_copy(x_hbm, x, x_sem)
     load_x.start()
-    chunks = [(m, e) for e in range(experts) for m in (0, 1)] + [(2, e) for e in range(experts)]
+    order = sorted(range(experts), key=lambda e: e not in hosted)
+    chunks = [(m, e) for e in order for m in (0, 1)] + [(2, e) for e in range(experts)]
+    everywhere = [k for k, (m, e) in enumerate(chunks) if m == 2 or e not in hosted]
+    feeds = [k for k, (m, e) in enumerate(chunks) if m < 2]
+    downs = [k for k, (m, e) in enumerate(chunks) if m == 2]
 
     def source(k):
         m, e = chunks[k]
@@ -74,21 +89,17 @@
 
     barrier = pltpu.get_barrier_semaphore()
     pl.semaphore_signal(barrier, inc=1, device_id=side, device_id_type=MESH)
+    pl.semaphore_signal(barrier, inc=1, device_id=inner, device_id_type=MESH)
     for i in range(1, tps):
         pl.semaphore_signal(
             barrier, inc=1, device_id=(dp, lax.rem(tp + i, tps)), device_id_type=MESH
         )
 
-    @pl.when(jnp.logical_not(top))
+    @pl.when(jnp.logical_not(end))
     def _():
-        pl.semaphore_signal(barrier, inc=1, device_id=above, device_id_type=MESH)
-
-    @pl.when(jnp.logical_not(bottom))
-    def _():
-        pl.semaphore_signal(barrier, inc=1, device_id=below, device_id_type=MESH)
-
-    ends = jnp.where(top, 1, 0) + jnp.where(bottom, 1, 0)
-    pl.semaphore_wait(barrier, tps + 2 - ends)
+        pl.semaphore_signal(barrier, inc=1, device_id=outer, device_id_type=MESH)
+
+    pl.semaphore_wait(barrier, tps + 2 - jnp.where(end, 1, 0))
 
     def send(k, d, src, sem, to):
         return pltpu.make_async_remote_copy(
@@ -97,62 +108,49 @@
         )
 
     def arrived(k, d):
-        pltpu.make_async_remote_copy(
-            src_ref=slot(k, d), dst_ref=slot(k, d), send_sem=side_sem.at[k, d // CORES],
-            recv_sem=recv_sem.at[k, d], device_id=side, device_id_type=MESH,
-        ).wait_recv()
-
-    def send_own(k):
-        @pl.when(jnp.logical_not(top))
-        def _():
-            send(k, dp, source(k), up_sem, above).start()
-
-        @pl.when(jnp.logical_not(bottom))
-        def _():
-            send(k, dp, source(k), down_sem, below).start()
-
-        send(k, dp, source(k), side_sem, side).start()
-
-    def relay(k):
-        for j in range(1, positions):
-            @pl.when(z - j >= 0)
-            def _():
-                d = dp - j * CORES
-                arrived(k, d)
-
-                @pl.when(jnp.logical_not(top))
-                def _():
-                    send(k, d, slot(k, d), up_sem, above).start()
-
-                send(k, d, slot(k, d), side_sem, side).start()
-
-            @pl.when(z + j <= positions - 1)
-            def _():
-                d = dp + j * CORES
-                arrived(k, d)
-
-                @pl.when(jnp.logical_not(bottom))
-                def _():
-                    send(k, d, slot(k, d), down_sem, below).start()
-
-                send(k, d, slot(k, d), side_sem, side).start()
+        send(k, d, slot(k, d), side_sem, side).wait_recv()
+
+    def pass_on(k, p, targets):
+        d = p * CORES + core
+        arrived(k, d)
+        for sem, to in targets:
+            send(k, d, slot(k, d), sem, to).start()
 
     def wait_side(k):
         for p in range(positions):
             arrived(k, p * CORES + (1 - core))
         copy_own(k).wait()
 
-    def norm():
-        step = rows // 8
+    quarter = rows // tps
+    piece = quarter // PIECES
+
+    def token_part(q, p):
+        return pl.ds(pl.multiple_of(q * quarter + p * piece, piece), piece)
+
+    def token_copy(src, q, p, kind, to):
+        return pltpu.make_async_remote_copy(
+            src_ref=src.at[token_part(q, p)], dst_ref=guest.at[token_part(q, p)],
+            send_sem=tok_send.at[kind, p], recv_sem=tok_recv.at[q, p],
+            device_id=to, device_id_type=MESH,
+        )
+
+    def token_arrived(q, p):
+        token_copy(guest, q, p, 0, side).wait_recv()
+
+    def norm(src, dst, start, count, steps):
+        step = count // steps
 
         def body(i, _):
-            part = pl.ds(pl.multiple_of(i * step, step), step)
-            v = x[part, :].astype(jnp.float32)
+            part = pl.ds(pl.multiple_of(start + i * step, step), step)
+            v = src[part, :].astype(jnp.float32)
             square = jnp.mean(v * v, axis=-1, keepdims=True)
-            x[part, :] = (v * lax.rsqrt(square + EPS) * gain_ref[...]).astype(jnp.bfloat16)
+            dst[part, :] = (v * lax.rsqrt(square + EPS) * gain_ref[...]).astype(jnp.bfloat16)
             return 0
 
-        lax.fori_loop(0, 8, body, 0)
+        lax.fori_loop(0, steps, body, 0)
+
+    def norm_quarter(q):
+        norm(guest, guest_normed, q * quarter, quarter, 2)
 
     def score():
         rest = router_ref[...]
@@ -184,12 +182,22 @@
             device_id=(dp, lax.rem(tp + i, tps)), device_id_type=MESH,
         )
 
-    def experts_hidden(e):
+    def share_hidden(e):
+        for i in range(1, tps):
+            send_hidden(e, i).start()
+
+    def send_back(e):
+        return pltpu.make_async_remote_copy(
+            src_ref=guest_hid.at[e], dst_ref=hid.at[e, tp], send_sem=back_send.at[e],
+            recv_sem=back_recv.at[e], device_id=outer, device_id_type=MESH,
+        )
+
+    def expert_hidden(e, src, dst):
         step = rows // 2
 
         def body(i, _):
             part = pl.ds(pl.multiple_of(i * step, step), step)
-            lhs = x[part, :]
+            lhs = src[part, :]
             depth = x.shape[1]
             gate = jnp.dot(
                 lhs, w[0, e].reshape(depth, w.shape[-1]), preferred_element_type=jnp.float32
@@ -197,12 +205,23 @@
             up = jnp.dot(
                 lhs, w[1, e].reshape(depth, w.shape[-1]), preferred_element_type=jnp.float32
             )
-            hid[e, tp, part, :] = (gate / (1.0 + jnp.exp(-gate)) * up).astype(jnp.bfloat16)
+            dst[part, :] = (gate / (1.0 + jnp.exp(-gate)) * up).astype(jnp.bfloat16)
             return 0
 
         lax.fori_loop(0, 2, body, 0)
-        for i in range(1, tps):
-            send_hidden(e, i).start()
+
+    def own_hidden(e):
+        expert_hidden(e, x, hid.at[e, tp])
+        share_hidden(e)
+
+    def guest_hidden(e):
+        expert_hidden(e, guest_normed, guest_hid.at[e])
+        send_back(e).start()
+
+    def sides_of(e):
+        for k in feeds:
+            if chunks[k][1] == e:
+                wait_side(k)
 
     def down():
         cols = o_ref.shape[1]
@@ -222,27 +241,108 @@
 
         lax.fori_loop(0, 4, body, 0)
 
-    ahead = 2
-    for k in range(min(ahead, len(chunks))):
-        send_own(k)
-    for k in range(len(chunks)):
-        relay(k)
-        if k + ahead < len(chunks):
-            send_own(k + ahead)
-        m, e = chunks[k]
-        if k == 0:
-            load_x.wait()
-            norm()
-        if k == 2:
-            score()
-        if m == 1:
-            wait_side(k - 1)
-            wait_side(k)
-            experts_hidden(e)
-    for k, (m, e) in enumerate(chunks):
-        if m == 2:
-            wait_side(k)
-    for e in range(experts):
+    to_in, to_out, to_side = (in_sem, inner), (out_sem, outer), (side_sem, side)
+
+    @pl.when(end)
+    def _():
+        for p in range(PIECES):
+            token_copy(x_hbm, tp, p, 0, inner).start()
+        for k in range(len(chunks)):
+            send(k, dp, source(k), *to_in).start()
+        for k in everywhere:
+            send(k, dp, source(k), *to_side).start()
+        load_x.wait()
+        norm(x, x, 0, rows, 8)
+        score()
+        for j in range(1, positions - 1):
+            for k in everywhere:
+                pass_on(k, z - j * out, [to_side])
+        for e in order:
+            if e in hosted:
+                send_back(e).wait_recv()
+                share_hidden(e)
+        for e in order:
+            if e not in hosted:
+                for k in feeds:
+                    if chunks[k][1] == e:
+                        pass_on(k, z - (positions - 1) * out, [to_side])
+                sides_of(e)
+                own_hidden(e)
+        for k in downs:
+            pass_on(k, z - (positions - 1) * out, [to_side])
+        for k in range(len(chunks)):
+            if k not in everywhere:
+                copy_own(k).wait()
+
+    @pl.when(jnp.logical_not(end))
+    def _():
+        def beyond(k):
+            return [to_out] if k in everywhere else []
+
+        for k in range(len(chunks)):
+            send(k, dp, source(k), *to_in).start()
+        for k in everywhere:
+            send(k, dp, source(k), *to_out).start()
+        for k in range(len(chunks)):
+            send(k, dp, source(k), *to_side).start()
+
+        def from_outer(k):
+            pass_on(k, z + out, [to_in, to_side])
+
+        def from_near(k):
+            pass_on(k, z - out, beyond(k) + [to_side])
+
+        def from_far(k):
+            pass_on(k, z - 2 * out, beyond(k) + [to_side])
+
+        load_x.wait()
+        norm(x, x, 0, rows, 8)
+        for p in range(PIECES):
+            token_arrived(tp, p)
+            token_copy(guest, tp, p, 0, (dp, along_x)).start()
+            token_copy(guest, tp, p, 1, (dp, along_y)).start()
+            from_near(p)
+        norm_quarter(tp)
+        for p in range(PIECES):
+            token_arrived(along_x, p)
+            if p < PIECES // 2:
+                token_copy(guest, along_x, p, 2, (dp, along_y)).start()
+            token_arrived(along_y, p)
+            if p >= PIECES // 2:
+                token_copy(guest, along_y, p, 2, (dp, along_x)).start()
+            if p == 1:
+                score()
+                for k in downs:
+                    from_near(k)
+            if p == 2:
+                from_outer(feeds[0])
+        from_outer(feeds[1])
+        norm_quarter(along_x)
+        norm_quarter(along_y)
+        from_far(feeds[0])
+        from_outer(feeds[2])
+        for p in range(PIECES):
+            token_arrived(across, p)
+        norm_quarter(across)
+        from_far(feeds[1])
+        from_outer(feeds[3])
+        sides_of(order[0])
+        guest_hidden(order[0])
+        from_outer(downs[0])
+        from_far(feeds[2])
+        own_hidden(order[0])
+        from_outer(downs[1])
+        from_far(feeds[3])
+        sides_of(order[1])
+        if order[1] in hosted:
+            guest_hidden(order[1])
+        own_hidden(order[1])
+        for k in downs:
+            from_far(k)
+
+    for k in downs:
+        wait_side(k)
+    for e in order:
         for i in range(1, tps):
             s = lax.rem(tp + i, tps)
             pltpu.make_async_remote_copy(
@@ -251,21 +351,39 @@
             ).wait_recv()
     down()
 
+    def sent(k, p, sem):
+        d = p * CORES + core
+        send(k, d, slot(k, d), sem, side).wait_send()
+
     for e in range(experts):
         for i in range(1, tps):
             send_hidden(e, i).wait_send()
     for k in range(len(chunks)):
-        for p in range(positions):
-            d = p * CORES + core
-            send(k, d, slot(k, d), side_sem, side).wait_send()
-
-            @pl.when(jnp.logical_and(jnp.logical_not(top), p <= z))
-            def _():
-                send(k, d, slot(k, d), up_sem, above).wait_send()
-
-            @pl.when(jnp.logical_and(jnp.logical_not(bottom), p >= z))
-            def _():
-                send(k, d, slot(k, d), down_sem, below).wait_send()
+        sent(k, z, in_sem)
+
+    @pl.when(end)
+    def _():
+        for p in range(PIECES):
+            token_copy(x_hbm, tp, p, 0, inner).wait_send()
+        for k in everywhere:
+            for p in range(positions):
+                sent(k, p, side_sem)
+
+    @pl.when(jnp.logical_not(end))
+    def _():
+        for p in range(PIECES):
+            for kind in range(3):
+                token_copy(guest, tp, p, kind, side).wait_send()
+        for e in hosted:
+            send_back(e).wait_send()
+        for k in range(len(chunks)):
+            sent(k, z + out, in_sem)
+            for p in range(positions):
+                sent(k, p, side_sem)
+        for k in everywhere:
+            sent(k, z, out_sem)
+            sent(k, z - out, out_sem)
+            sent(k, z - 2 * out, out_sem)
 
 
 def streamed(groups, tps, tokens, gain, router, routes, w_gate, w_up, w_down):
@@ -278,15 +396,18 @@
     chunks = 3 * experts
     dma = pltpu.SemaphoreType.DMA
     return pl.pallas_call(
-        functools.partial(kernel, groups, tps),
+        functools.partial(kernel, groups, tps, HOSTED),
         out_shape=jax.ShapeDtypeStruct((rows, cols), jnp.bfloat16),
         in_specs=[hbm, vmem, vmem, vmem, hbm, hbm, hbm],
         out_specs=vmem,
         scratch_shapes=[
             pltpu.VMEM((rows, depth), jnp.bfloat16),
+            pltpu.VMEM((rows, depth), jnp.bfloat16),
+            pltpu.VMEM((rows, depth), jnp.bfloat16),
             pltpu.VMEM((2, experts, groups, shard, width), jnp.bfloat16),
             pltpu.VMEM((experts, groups, down_rows, cols), jnp.bfloat16),
             pltpu.VMEM((experts, tps, rows, width), jnp.bfloat16),
+            pltpu.VMEM((experts, rows, width), jnp.bfloat16),
             pltpu.VMEM((rows, router.shape[1]), jnp.float32),
             dma,
             dma((chunks,)),
@@ -296,6 +417,10 @@
             dma((chunks, positions)),
             dma((experts, tps - 1)),
             dma((experts, tps)),
+            dma((3, PIECES)),
+            dma((tps, PIECES)),
+            dma((experts,)),
+            dma((experts,)),
         ],
         compiler_params=pltpu.CompilerParams(
             collective_id=0, has_side_effects=True, vmem_limit_bytes=60 * 1024 * 1024
@@ -305,7 +430,7 @@
 
 def solution(mesh):
     groups, tps = mesh.shape["dp"], mesh.shape["tp"]
-    fits = groups % CORES == 0 and groups // CORES <= 4
+    fits = groups == 4 * CORES and tps == 4
     body = functools.partial(streamed, groups, tps) if fits else gathered
     return jax.shard_map(
         body,

time: 118 us -> 101 us (0.86)
  Pallas kernels: 115 us -> 98.3 us
    pallas_call x1, Pallas kernels: 115 us -> 98.3 us  [streamed(): pl.pallas_call(functools.partial(kernel, groups, tps, HOSTED), out_shape=...]
where the time goes in v2:
time: 101 us
  Pallas kernels  98.3 us (97%)
  local copies, waits for them, and re-layouts  2.26 us (2%)
    pallas_call x1, Pallas kernels, streamed(): pl.pallas_call(functools.partial(kernel, groups, tps, HOSTED), out_shape=...  98.3 us
    unnamed x1, local copies, waits for them, and re-layouts  2.26 us

profile of v2, /device:TPU:0, one launch (start us, length us, event | category | flops | bytes accessed | tf_op | source)
XLA Modules:
  0.0 100.5 jit_solution(3287366994776308792)
XLA Ops:
  0.0 98.3 %shard_map.73 = bf16[512,1024]{1,0:T(8,128)(2,1)} custom-call(bf16[512,4096]{1,0:T(8,128)(2,1)} %x_hbm.1, f32[1,4096]{1,0:T(1,128)} %bitcast.4, f32[8,4096]{1,0:T(8,128)} %bitcast.3, s32[2,512]{1,0:T(2,128)} %bitcast.5, bf16[2,512,256]{2,1,0:T(8,128)(2,1)} %wg_hbm.1, bf16[2,512,256]{2,1,0:T(8,128)(2,1)} %wu_hbm.1, bf16[2,128,1024]{2,1,0:T(8,128)(2,1)} %wd_hbm.1), custom_call_target="tpu_custom_call" | custom-call | tf_op jit(solution)/shard_map/pallas_call | solution.py:398
  98.3 2.3 %copy.9 = bf16[512,1024]{1,0:T(8,128)(2,1)} copy(bf16[512,1024]{1,0:T(8,128)(2,1)} %shard_map.73) | data formatting | bytes 2097152

commit v3 on v2

--- a/solution.py
+++ b/solution.py
@@ -12,7 +12,7 @@
 MESH = pl.DeviceIdType.MESH
 CORES = 2
 PIECES = 4
-HOSTED = (0,)
+HOSTED = (0, 1)
 
 
 def gathered(tokens, gain, router, routes, w_gate, w_up, w_down):

time: 101 us -> 96.8 us (0.958)
  Pallas kernels: 98.3 us -> 94.4 us
    pallas_call x1, Pallas kernels: 98.3 us -> 94.4 us  [streamed(): pl.pallas_call(functools.partial(kernel, groups, tps, HOSTED), out_shape=...]
where the time goes in v3:
time: 96.8 us; the launch traced here: 96.7 us
  Pallas kernels  94.4 us (98%)
  local copies, waits for them, and re-layouts  2.26 us (2%)
    pallas_call x1, Pallas kernels, streamed(): pl.pallas_call(functools.partial(kernel, groups, tps, HOSTED), out_shape=...  94.4 us
    unnamed x1, local copies, waits for them, and re-layouts  2.26 us

profile of v3, /device:TPU:0, one launch (start us, length us, event | category | flops | bytes accessed | tf_op | source)
XLA Modules:
  0.0 96.7 jit_solution(12134697374242135262)
XLA Ops:
  0.0 94.4 %shard_map.73 = bf16[512,1024]{1,0:T(8,128)(2,1)} custom-call(bf16[512,4096]{1,0:T(8,128)(2,1)} %x_hbm.1, f32[1,4096]{1,0:T(1,128)} %bitcast.4, f32[8,4096]{1,0:T(8,128)} %bitcast.3, s32[2,512]{1,0:T(2,128)} %bitcast.5, bf16[2,512,256]{2,1,0:T(8,128)(2,1)} %wg_hbm.1, bf16[2,512,256]{2,1,0:T(8,128)(2,1)} %wu_hbm.1, bf16[2,128,1024]{2,1,0:T(8,128)(2,1)} %wd_hbm.1), custom_call_target="tpu_custom_call" | custom-call | tf_op jit(solution)/shard_map/pallas_call | solution.py:398
  94.4 2.3 %copy.9 = bf16[512,1024]{1,0:T(8,128)(2,1)} copy(bf16[512,1024]{1,0:T(8,128)(2,1)} %shard_map.73) | data formatting | bytes 2097152

commit v4 on v3

--- a/solution.py
+++ b/solution.py
@@ -12,6 +12,7 @@
 MESH = pl.DeviceIdType.MESH
 CORES = 2
 PIECES = 4
+HALVES = 2
 HOSTED = (0, 1)
 
 
@@ -43,7 +44,7 @@
 
 def kernel(
     groups, tps, hosted, x_hbm, gain_ref, router_ref, routes_ref, wg_hbm, wu_hbm, wd_hbm, o_ref,
-    x, guest, guest_normed, w, dn, hid, guest_hid, comb,
+    x, guest, guest_normed, w, dn, hid, guest_hid, comb, total,
     x_sem, own_sem, recv_sem, in_sem, out_sem, side_sem, hid_send, hid_recv,
     tok_send, tok_recv, back_send, back_recv,
 ):
@@ -68,18 +69,21 @@
     load_x = pltpu.make_async_copy(x_hbm, x, x_sem)
     load_x.start()
     order = sorted(range(experts), key=lambda e: e not in hosted)
-    chunks = [(m, e) for e in order for m in (0, 1)] + [(2, e) for e in range(experts)]
-    everywhere = [k for k, (m, e) in enumerate(chunks) if m == 2 or e not in hosted]
-    feeds = [k for k, (m, e) in enumerate(chunks) if m < 2]
-    downs = [k for k, (m, e) in enumerate(chunks) if m == 2]
+    chunks = [(m, e, 0) for e in order for m in (0, 1)]
+    feeds = list(range(len(chunks)))
+    chunks += [(2, e, h) for e in order for h in range(HALVES)]
+    downs = [k for k in range(len(chunks)) if k not in feeds]
+    everywhere = [k for k, (m, e, _) in enumerate(chunks) if m == 2 or e not in hosted]
+    half = dn.shape[2] // HALVES
+    strip = rows // HALVES
 
     def source(k):
-        m, e = chunks[k]
-        return (wg_hbm, wu_hbm, wd_hbm)[m].at[e]
+        m, e, h = chunks[k]
+        return wd_hbm.at[e, pl.ds(h * half, half)] if m == 2 else (wg_hbm, wu_hbm)[m].at[e]
 
     def slot(k, d):
-        m, e = chunks[k]
-        return dn.at[e, d] if m == 2 else w.at[m, e, d]
+        m, e, h = chunks[k]
+        return dn.at[e, d, pl.ds(h * half, half)] if m == 2 else w.at[m, e, d]
 
     def copy_own(k):
         return pltpu.make_async_copy(source(k), slot(k, dp), own_sem.at[k])
@@ -154,17 +158,17 @@
 
     def score():
         rest = router_ref[...]
-        total = jnp.zeros((rows, rest.shape[0]), jnp.float32)
+        logits = jnp.zeros((rows, rest.shape[0]), jnp.float32)
         parts = []
         for _ in range(3):
             part = rest.astype(jnp.bfloat16)
             rest = rest - part.astype(jnp.float32)
             parts.append(part)
         for part in parts[::-1]:
-            total += lax.dot_general(
+            logits += lax.dot_general(
                 x[...], part, (((1,), (1,)), ((), ())), preferred_element_type=jnp.float32
             )
-        scores = 1.0 / (1.0 + jnp.exp(-total))
+        scores = 1.0 / (1.0 + jnp.exp(-logits))
         routed = scores.shape[1]
         picks = routes_ref[...].astype(jnp.float32)
         labels = lax.broadcasted_iota(jnp.int32, scores.shape, 1).astype(jnp.float32)
@@ -175,68 +179,84 @@
         picked = chosen * scores
         comb[...] = picked * ROUTE_SCALE / jnp.sum(picked, axis=-1, keepdims=True)
 
-    def send_hidden(e, i):
+    def send_hidden(e, h, i):
+        part = pl.ds(h * strip, strip)
         return pltpu.make_async_remote_copy(
-            src_ref=hid.at[e, tp], dst_ref=hid.at[e, tp], send_sem=hid_send.at[e, i - 1],
-            recv_sem=hid_recv.at[e, tp],
+            src_ref=hid.at[e, tp, part], dst_ref=hid.at[e, tp, part],
+            send_sem=hid_send.at[e, h, i - 1], recv_sem=hid_recv.at[e, h, tp],
             device_id=(dp, lax.rem(tp + i, tps)), device_id_type=MESH,
         )
 
-    def share_hidden(e):
+    def share_hidden(e, h):
         for i in range(1, tps):
-            send_hidden(e, i).start()
-
-    def send_back(e):
+            send_hidden(e, h, i).start()
+
+    def wait_hidden(e):
+        for h in range(HALVES):
+            part = pl.ds(h * strip, strip)
+            for i in range(1, tps):
+                s = lax.rem(tp + i, tps)
+                pltpu.make_async_remote_copy(
+                    src_ref=hid.at[e, s, part], dst_ref=hid.at[e, s, part],
+                    send_sem=hid_send.at[e, h, i - 1], recv_sem=hid_recv.at[e, h, s],
+                    device_id=side, device_id_type=MESH,
+                ).wait_recv()
+
+    def send_back(e, h):
+        part = pl.ds(h * strip, strip)
         return pltpu.make_async_remote_copy(
-            src_ref=guest_hid.at[e], dst_ref=hid.at[e, tp], send_sem=back_send.at[e],
-            recv_sem=back_recv.at[e], device_id=outer, device_id_type=MESH,
-        )
-
-    def expert_hidden(e, src, dst):
-        step = rows // 2
-
-        def body(i, _):
-            part = pl.ds(pl.multiple_of(i * step, step), step)
-            lhs = src[part, :]
-            depth = x.shape[1]
-            gate = jnp.dot(
-                lhs, w[0, e].reshape(depth, w.shape[-1]), preferred_element_type=jnp.float32
-            )
-            up = jnp.dot(
-                lhs, w[1, e].reshape(depth, w.shape[-1]), preferred_element_type=jnp.float32
-            )
-            dst[part, :] = (gate / (1.0 + jnp.exp(-gate)) * up).astype(jnp.bfloat16)
-            return 0
-
-        lax.fori_loop(0, 2, body, 0)
+            src_ref=guest_hid.at[e, part], dst_ref=hid.at[e, tp, part],
+            send_sem=back_send.at[e, h], recv_sem=back_recv.at[e, h],
+            device_id=outer, device_id_type=MESH,
+        )
+
+    def expert_hidden(e, h, src, dst):
+        part = pl.ds(h * strip, strip)
+        lhs = src[part, :]
+        depth = x.shape[1]
+        gate = jnp.dot(
+            lhs, w[0, e].reshape(depth, w.shape[-1]), preferred_element_type=jnp.float32
+        )
+        up = jnp.dot(
+            lhs, w[1, e].reshape(depth, w.shape[-1]), preferred_element_type=jnp.float32
+        )
+        dst[part, :] = (gate / (1.0 + jnp.exp(-gate)) * up).astype(jnp.bfloat16)
 
     def own_hidden(e):
-        expert_hidden(e, x, hid.at[e, tp])
-        share_hidden(e)
+        for h in range(HALVES):
+            expert_hidden(e, h, x, hid.at[e, tp])
+            share_hidden(e, h)
 
     def guest_hidden(e):
-        expert_hidden(e, guest_normed, guest_hid.at[e])
-        send_back(e).start()
+        for h in range(HALVES):
+            expert_hidden(e, h, guest_normed, guest_hid.at[e])
+            send_back(e, h).start()
 
     def sides_of(e):
         for k in feeds:
             if chunks[k][1] == e:
                 wait_side(k)
 
-    def down():
+    def down(e):
         cols = o_ref.shape[1]
         step = cols // 4
+        wait_hidden(e)
+        for k in downs:
+            if chunks[k][1] == e:
+                wait_side(k)
 
         def body(i, _):
             part = pl.ds(pl.multiple_of(i * step, step), step)
-            total = None
-            for e in range(experts):
-                lhs = jnp.concatenate([hid[e, t] for t in range(tps)], axis=1)
-                rhs = dn[e, :, :, part].reshape(lhs.shape[1], step)
-                term = jnp.dot(lhs, rhs, preferred_element_type=jnp.float32)
-                term = term * comb[:, e : e + 1]
-                total = term if total is None else total + term
-            o_ref[:, part] = total.astype(o_ref.dtype)
+            lhs = jnp.concatenate([hid[e, t] for t in range(tps)], axis=1)
+            rhs = dn[e, :, :, part].reshape(lhs.shape[1], step)
+            term = jnp.dot(lhs, rhs, preferred_element_type=jnp.float32)
+            term = term * comb[:, e : e + 1]
+            if e != order[0]:
+                term += total[:, part]
+            if e == order[-1]:
+                o_ref[:, part] = term.astype(o_ref.dtype)
+            else:
+                total[:, part] = term
             return 0
 
         lax.fori_loop(0, 4, body, 0)
@@ -254,22 +274,28 @@
         load_x.wait()
         norm(x, x, 0, rows, 8)
         score()
-        for j in range(1, positions - 1):
-            for k in everywhere:
-                pass_on(k, z - j * out, [to_side])
+        for k in everywhere:
+            pass_on(k, z - out, [to_side])
+        for k in everywhere[:-1]:
+            pass_on(k, z - 2 * out, [to_side])
         for e in order:
             if e in hosted:
-                send_back(e).wait_recv()
-                share_hidden(e)
+                for h in range(HALVES):
+                    send_back(e, h).wait_recv()
+                    share_hidden(e, h)
+        pass_on(everywhere[-1], z - 2 * out, [to_side])
         for e in order:
             if e not in hosted:
                 for k in feeds:
                     if chunks[k][1] == e:
-                        pass_on(k, z - (positions - 1) * out, [to_side])
+                        pass_on(k, z - 3 * out, [to_side])
                 sides_of(e)
                 own_hidden(e)
-        for k in downs:
-            pass_on(k, z - (positions - 1) * out, [to_side])
+        for e in order:
+            for k in downs:
+                if chunks[k][1] == e:
+                    pass_on(k, z - 3 * out, [to_side])
+            down(e)
         for k in range(len(chunks)):
             if k not in everywhere:
                 copy_own(k).wait()
@@ -279,7 +305,7 @@
         def beyond(k):
             return [to_out] if k in everywhere else []
 
-        for k in range(len(chunks)):
+        for k in range(len(chunks) - 1):
             send(k, dp, source(k), *to_in).start()
         for k in everywhere:
             send(k, dp, source(k), *to_out).start()
@@ -310,10 +336,12 @@
             token_arrived(along_y, p)
             if p >= PIECES // 2:
                 token_copy(guest, along_y, p, 2, (dp, along_x)).start()
+            if p == 0:
+                from_near(downs[0])
+                from_near(downs[1])
             if p == 1:
                 score()
-                for k in downs:
-                    from_near(k)
+                from_near(downs[2])
             if p == 2:
                 from_outer(feeds[0])
         from_outer(feeds[1])
@@ -321,43 +349,40 @@
         norm_quarter(along_y)
         from_far(feeds[0])
         from_outer(feeds[2])
+        from_far(feeds[1])
         for p in range(PIECES):
             token_arrived(across, p)
         norm_quarter(across)
-        from_far(feeds[1])
         from_outer(feeds[3])
+        send(len(chunks) - 1, dp, source(len(chunks) - 1), *to_in).start()
         sides_of(order[0])
         guest_hidden(order[0])
+        from_far(feeds[2])
         from_outer(downs[0])
-        from_far(feeds[2])
         own_hidden(order[0])
         from_outer(downs[1])
         from_far(feeds[3])
         sides_of(order[1])
         if order[1] in hosted:
             guest_hidden(order[1])
+        from_outer(downs[2])
+        from_near(downs[3])
         own_hidden(order[1])
-        for k in downs:
-            from_far(k)
-
-    for k in downs:
-        wait_side(k)
-    for e in order:
-        for i in range(1, tps):
-            s = lax.rem(tp + i, tps)
-            pltpu.make_async_remote_copy(
-                src_ref=hid.at[e, s], dst_ref=hid.at[e, s], send_sem=hid_send.at[e, i - 1],
-                recv_sem=hid_recv.at[e, s], device_id=side, device_id_type=MESH,
-            ).wait_recv()
-    down()
+        from_outer(downs[3])
+        for e in order:
+            for k in downs:
+                if chunks[k][1] == e:
+                    from_far(k)
+            down(e)
 
     def sent(k, p, sem):
         d = p * CORES + core
         send(k, d, slot(k, d), sem, side).wait_send()
 
     for e in range(experts):
-        for i in range(1, tps):
-            send_hidden(e, i).wait_send()
+        for h in range(HALVES):
+            for i in range(1, tps):
+                send_hidden(e, h, i).wait_send()
     for k in range(len(chunks)):
         sent(k, z, in_sem)
 
@@ -375,7 +400,8 @@
             for kind in range(3):
                 token_copy(guest, tp, p, kind, side).wait_send()
         for e in hosted:
-            send_back(e).wait_send()
+            for h in range(HALVES):
+                send_back(e, h).wait_send()
         for k in range(len(chunks)):
             sent(k, z + out, in_sem)
             for p in range(positions):
@@ -393,7 +419,7 @@
     positions = groups // CORES
     vmem = pl.BlockSpec(memory_space=pltpu.VMEM)
     hbm = pl.BlockSpec(memory_space=pl.ANY)
-    chunks = 3 * experts
+    chunks = (2 + HALVES) * experts
     dma = pltpu.SemaphoreType.DMA
     return pl.pallas_call(
         functools.partial(kernel, groups, tps, HOSTED),
@@ -409,18 +435,19 @@
             pltpu.VMEM((experts, tps, rows, width), jnp.bfloat16),
             pltpu.VMEM((experts, rows, width), jnp.bfloat16),
             pltpu.VMEM((rows, router.shape[1]), jnp.float32),
+            pltpu.VMEM((rows, cols), jnp.float32),
             dma,
             dma((chunks,)),
             dma((chunks, groups)),
             dma((chunks, positions)),
             dma((chunks, positions)),
             dma((chunks, positions)),
-            dma((experts, tps - 1)),
-            dma((experts, tps)),
+            dma((experts, HALVES, tps - 1)),
+            dma((experts, HALVES, tps)),
             dma((3, PIECES)),
             dma((tps, PIECES)),
-            dma((experts,)),
-            dma((experts,)),
+            dma((experts, HALVES)),
+            dma((experts, HALVES)),
         ],
         compiler_params=pltpu.CompilerParams(
             collective_id=0, has_side_effects=True, vmem_limit_bytes=60 * 1024 * 1024

time: 96.8 us -> 99.6 us (1.029)
  Pallas kernels: 94.4 us -> 97.1 us
    pallas_call x1, Pallas kernels: 94.4 us -> 97.1 us  [streamed(): pl.pallas_call(functools.partial(kernel, groups, tps, HOSTED), out_shape=...]
where the time goes in v4:
time: 99.6 us; the launch traced here: 99.4 us
  Pallas kernels  97.1 us (97%)
  local copies, waits for them, and re-layouts  2.26 us (2%)
    pallas_call x1, Pallas kernels, streamed(): pl.pallas_call(functools.partial(kernel, groups, tps, HOSTED), out_shape=...  97.1 us
    unnamed x1, local copies, waits for them, and re-layouts  2.26 us

profile of v4, /device:TPU:0, one launch (start us, length us, event | category | flops | bytes accessed | tf_op | source)
XLA Modules:
  0.0 99.4 jit_solution(7030620782325375914)
XLA Ops:
  0.0 97.1 %shard_map.73 = bf16[512,1024]{1,0:T(8,128)(2,1)} custom-call(bf16[512,4096]{1,0:T(8,128)(2,1)} %x_hbm.1, f32[1,4096]{1,0:T(1,128)} %bitcast.4, f32[8,4096]{1,0:T(8,128)} %bitcast.3, s32[2,512]{1,0:T(2,128)} %bitcast.5, bf16[2,512,256]{2,1,0:T(8,128)(2,1)} %wg_hbm.1, bf16[2,512,256]{2,1,0:T(8,128)(2,1)} %wu_hbm.1, bf16[2,128,1024]{2,1,0:T(8,128)(2,1)} %wd_hbm.1), custom_call_target="tpu_custom_call" | custom-call | tf_op jit(solution)/shard_map/pallas_call | solution.py:424
  97.1 2.3 %copy.9 = bf16[512,1024]{1,0:T(8,128)(2,1)} copy(bf16[512,1024]{1,0:T(8,128)(2,1)} %shard_map.73) | data formatting | bytes 2097152

commit v5 on v4

--- a/solution.py
+++ b/solution.py
@@ -179,28 +179,26 @@
         picked = chosen * scores
         comb[...] = picked * ROUTE_SCALE / jnp.sum(picked, axis=-1, keepdims=True)
 
-    def send_hidden(e, h, i):
+    def hidden_copy(e, h, t, kind, to):
         part = pl.ds(h * strip, strip)
         return pltpu.make_async_remote_copy(
-            src_ref=hid.at[e, tp, part], dst_ref=hid.at[e, tp, part],
-            send_sem=hid_send.at[e, h, i - 1], recv_sem=hid_recv.at[e, h, tp],
-            device_id=(dp, lax.rem(tp + i, tps)), device_id_type=MESH,
+            src_ref=hid.at[e, t, part], dst_ref=hid.at[e, t, part],
+            send_sem=hid_send.at[e, h, kind], recv_sem=hid_recv.at[e, h, t],
+            device_id=(dp, to), device_id_type=MESH,
         )
 
     def share_hidden(e, h):
-        for i in range(1, tps):
-            send_hidden(e, h, i).start()
+        hidden_copy(e, h, tp, 0, along_x).start()
+        hidden_copy(e, h, tp, 1, along_y).start()
+
+    def relay_hidden(e):
+        for h, (t, to) in enumerate(((along_x, along_y), (along_y, along_x))):
+            hidden_copy(e, h, t, 2, to).wait_recv()
+            hidden_copy(e, h, t, 2, to).start()
 
     def wait_hidden(e):
-        for h in range(HALVES):
-            part = pl.ds(h * strip, strip)
-            for i in range(1, tps):
-                s = lax.rem(tp + i, tps)
-                pltpu.make_async_remote_copy(
-                    src_ref=hid.at[e, s, part], dst_ref=hid.at[e, s, part],
-                    send_sem=hid_send.at[e, h, i - 1], recv_sem=hid_recv.at[e, h, s],
-                    device_id=side, device_id_type=MESH,
-                ).wait_recv()
+        for h, t in ((0, along_y), (1, along_x), (0, across), (1, across)):
+            hidden_copy(e, h, t, 2, along_x).wait_recv()
 
     def send_back(e, h):
         part = pl.ds(h * strip, strip)
@@ -283,6 +281,7 @@
                 for h in range(HALVES):
                     send_back(e, h).wait_recv()
                     share_hidden(e, h)
+                relay_hidden(e)
         pass_on(everywhere[-1], z - 2 * out, [to_side])
         for e in order:
             if e not in hosted:
@@ -291,6 +290,7 @@
                         pass_on(k, z - 3 * out, [to_side])
                 sides_of(e)
                 own_hidden(e)
+                relay_hidden(e)
         for e in order:
             for k in downs:
                 if chunks[k][1] == e:
@@ -323,6 +323,7 @@
 
         load_x.wait()
         norm(x, x, 0, rows, 8)
+        score()
         for p in range(PIECES):
             token_arrived(tp, p)
             token_copy(guest, tp, p, 0, (dp, along_x)).start()
@@ -340,27 +341,27 @@
                 from_near(downs[0])
                 from_near(downs[1])
             if p == 1:
-                score()
                 from_near(downs[2])
             if p == 2:
                 from_outer(feeds[0])
+        norm_quarter(along_x)
         from_outer(feeds[1])
-        norm_quarter(along_x)
         norm_quarter(along_y)
         from_far(feeds[0])
         from_outer(feeds[2])
-        from_far(feeds[1])
         for p in range(PIECES):
             token_arrived(across, p)
         norm_quarter(across)
+        from_far(feeds[1])
+        sides_of(order[0])
+        own_hidden(order[0])
         from_outer(feeds[3])
         send(len(chunks) - 1, dp, source(len(chunks) - 1), *to_in).start()
-        sides_of(order[0])
         guest_hidden(order[0])
         from_far(feeds[2])
         from_outer(downs[0])
-        own_hidden(order[0])
         from_outer(downs[1])
+        relay_hidden(order[0])
         from_far(feeds[3])
         sides_of(order[1])
         if order[1] in hosted:
@@ -369,10 +370,11 @@
         from_near(downs[3])
         own_hidden(order[1])
         from_outer(downs[3])
+        from_far(downs[0])
+        relay_hidden(order[1])
+        for k in downs[1:]:
+            from_far(k)
         for e in order:
-            for k in downs:
-                if chunks[k][1] == e:
-                    from_far(k)
             down(e)
 
     def sent(k, p, sem):
@@ -381,8 +383,8 @@
 
     for e in range(experts):
         for h in range(HALVES):
-            for i in range(1, tps):
-                send_hidden(e, h, i).wait_send()
+            for kind in range(3):
+                hidden_copy(e, h, tp, kind, along_x).wait_send()
     for k in range(len(chunks)):
         sent(k, z, in_sem)
 
@@ -442,7 +444,7 @@
             dma((chunks, positions)),
             dma((chunks, positions)),
             dma((chunks, positions)),
-            dma((experts, HALVES, tps - 1)),
+            dma((experts, HALVES, 3)),
             dma((experts, HALVES, tps)),
             dma((3, PIECES)),
             dma((tps, PIECES)),

time: 99.6 us -> 97.3 us (0.977)
  Pallas kernels: 97.1 us -> 94.3 us
    pallas_call x1, Pallas kernels: 97.1 us -> 94.3 us  [streamed(): pl.pallas_call(functools.partial(kernel, groups, tps, HOSTED), out_shape=...]
where the time goes in v5:
time: 97.3 us; the launch traced here: 96.6 us
  Pallas kernels  94.3 us (97%)
  local copies, waits for them, and re-layouts  2.26 us (2%)
    pallas_call x1, Pallas kernels, streamed(): pl.pallas_call(functools.partial(kernel, groups, tps, HOSTED), out_shape=...  94.3 us
    unnamed x1, local copies, waits for them, and re-layouts  2.26 us

profile of v5, /device:TPU:0, one launch (start us, length us, event | category | flops | bytes accessed | tf_op | source)
XLA Modules:
  0.0 96.6 jit_solution(7463710405464298774)
XLA Ops:
  0.0 94.3 %shard_map.73 = bf16[512,1024]{1,0:T(8,128)(2,1)} custom-call(bf16[512,4096]{1,0:T(8,128)(2,1)} %x_hbm.1, f32[1,4096]{1,0:T(1,128)} %bitcast.4, f32[8,4096]{1,0:T(8,128)} %bitcast.3, s32[2,512]{1,0:T(2,128)} %bitcast.5, bf16[2,512,256]{2,1,0:T(8,128)(2,1)} %wg_hbm.1, bf16[2,512,256]{2,1,0:T(8,128)(2,1)} %wu_hbm.1, bf16[2,128,1024]{2,1,0:T(8,128)(2,1)} %wd_hbm.1), custom_call_target="tpu_custom_call" | custom-call | tf_op jit(solution)/shard_map/pallas_call | solution.py:426
  94.3 2.3 %copy.9 = bf16[512,1024]{1,0:T(8,128)(2,1)} copy(bf16[512,1024]{1,0:T(8,128)(2,1)} %shard_map.73) | data formatting | bytes 2097152

commit v6 on v5

--- a/solution.py
+++ b/solution.py
@@ -370,10 +370,9 @@
         from_near(downs[3])
         own_hidden(order[1])
         from_outer(downs[3])
-        from_far(downs[0])
+        for k in downs:
+            from_far(k)
         relay_hidden(order[1])
-        for k in downs[1:]:
-            from_far(k)
         for e in order:
             down(e)
 

time: 97.3 us -> 97.3 us (level)
  no operation moved by 1% of the time
where the time goes in v6:
time: 97.3 us; the launch traced here: 96.6 us
  Pallas kernels  94.3 us (97%)
  local copies, waits for them, and re-layouts  2.26 us (2%)
    pallas_call x1, Pallas kernels, streamed(): pl.pallas_call(functools.partial(kernel, groups, tps, HOSTED), out_shape=...  94.3 us
    unnamed x1, local copies, waits for them, and re-layouts  2.26 us

profile of v6, /device:TPU:0, one launch (start us, length us, event | category | flops | bytes accessed | tf_op | source)
XLA Modules:
  0.0 96.6 jit_solution(14799985520879443742)
XLA Ops:
  0.0 94.3 %shard_map.73 = bf16[512,1024]{1,0:T(8,128)(2,1)} custom-call(bf16[512,4096]{1,0:T(8,128)(2,1)} %x_hbm.1, f32[1,4096]{1,0:T(1,128)} %bitcast.4, f32[8,4096]{1,0:T(8,128)} %bitcast.3, s32[2,512]{1,0:T(2,128)} %bitcast.5, bf16[2,512,256]{2,1,0:T(8,128)(2,1)} %wg_hbm.1, bf16[2,512,256]{2,1,0:T(8,128)(2,1)} %wu_hbm.1, bf16[2,128,1024]{2,1,0:T(8,128)(2,1)} %wd_hbm.1), custom_call_target="tpu_custom_call" | custom-call | tf_op jit(solution)/shard_map/pallas_call | solution.py:425
  94.3 2.3 %copy.9 = bf16[512,1024]{1,0:T(8,128)(2,1)} copy(bf16[512,1024]{1,0:T(8,128)(2,1)} %shard_map.73) | data formatting | bytes 2097152
